TPU v7x, 32 devices: a whole 2x2x4 slice. The times are simulated.
32 devices in a mesh: dp: 4 (over x, core), band: 8 (over z, y).
Axes of the slice: x: 2, y: 2, z: 4, core: 2. Of those that a mesh axis runs over, the one named last changes fastest.
Arguments:
- features: bfloat16 [8160, 256], P(('dp', 'band')), parts along dimension 0, may hold values from -6 to 6
- corners: int32 [8160, 512], P(('dp', 'band')), parts along dimension 0, may hold values from 0 to 1535, as said below
- bilinear: float32 [8160, 512], P(('dp', 'band')), parts along dimension 0, may hold values from 0.08 to 0.5, as said below
- attention: float32 [8160, 128], P(('dp', 'band')), parts along dimension 0, may hold values from 0 to 1, as said below
- w_value: bfloat16 [256, 256], replicated, may hold values from -0.375 to 0.375
- b_value: float32 [256], replicated, may hold values from -0.6 to 0.6
- w_out: bfloat16 [256, 256], replicated, may hold values from -1.5 to 1.5
- b_out: float32 [256], replicated, may hold values from -3 to 3
- norm1_gain: float32 [256], replicated, may hold values from 0.5 to 1.5
- norm1_bias: float32 [256], replicated, may hold values from -3 to 3
- w_in: bfloat16 [256, 1024], replicated, may hold values from -0.375 to 0.375
- b_in: float32 [1024], replicated, may hold values from -3 to 3
- w_ffout: bfloat16 [1024, 256], replicated, may hold values from -0.1875 to 0.1875
- b_ffout: float32 [256], replicated, may hold values from -3 to 3
- norm2_gain: float32 [256], replicated, may hold values from 0.5 to 1.5
- norm2_bias: float32 [256], replicated, may hold values from -3 to 3
Outputs:
- encoded: bfloat16 [8160, 256], P(('dp', 'band')), parts along dimension 0
There are 4 independent parts, one for each index of `dp`. A program takes and returns all parts, laid end to end along the dimension named above; an argument that names none is the same for every part. Nothing has to cross between parts.
Inputs may be any that keep to these rules, and one draw needn't show every extreme that they name: An entry for level l is a row of a map of 192 * 8 // 4**l tokens laid out in rows of 128 // 2**l; the four corners of a point are k, k + 1, k + 128 // 2**l and k + 128 // 2**l + 1 in that order. `bilinear`: the four corner weights of a point are positive and sum to one. `attention`: for each token and head the 16 weights are positive and sum to one.
All inputs are finite; a program needn't handle non-finite values.
Results may differ from a plain program's by a relative error of at most 0.009.
Values may be sent and summed in bfloat16 or wider, within the bound.
A program may use at most 64 MiB of HBM per device.

v0:
```python
import jax
import jax.numpy as jnp
from jax import lax
from jax.sharding import PartitionSpec as P

HEADS = 8
LEVELS = 4
POINTS = 4
ROWS_DEV = 192


def layer_norm(inputs, gain, shift):
    average = jnp.mean(inputs, axis=-1, keepdims=True)
    centred = inputs - average
    variance = jnp.mean(centred * centred, axis=-1, keepdims=True)
    return centred * lax.rsqrt(variance + 1e-05) * gain + shift


def blend_rows(place_heads, weight_heads, value_block):
    row_count, model_width = value_block.shape
    head_dim = model_width // HEADS
    lane_groups = -(-row_count // 128)
    padding = lane_groups * 128 - row_count
    padded = jnp.pad(value_block, ((0, padding), (0, 0))).reshape(lane_groups, 128, HEADS, head_dim)
    per_head = jnp.transpose(padded, (2, 0, 1, 3))
    group_ids = jnp.arange(lane_groups, dtype=jnp.int32)
    lane_ids = jnp.arange(128, dtype=jnp.int32)

    def one_head(head_args):
        place_one, weight_one, value_one = head_args
        group_index = place_one // 128
        lane_index = place_one % 128
        group_hits = jnp.where(
            group_index[..., None] == group_ids, weight_one[..., None], jnp.zeros((), jnp.bfloat16)
        )
        lane_hits = (lane_index[..., None] == lane_ids).astype(jnp.bfloat16)
        hit_table = jnp.einsum(
            "qsa,qsb->qab", group_hits, lane_hits, preferred_element_type=jnp.float32
        )
        table_major = hit_table.astype(jnp.bfloat16)
        table_minor = (hit_table - table_major.astype(jnp.float32)).astype(jnp.bfloat16)
        result_major = jnp.einsum(
            "qab,abd->qd", table_major, value_one, preferred_element_type=jnp.float32
        )
        result_minor = jnp.einsum(
            "qab,abd->qd", table_minor, value_one, preferred_element_type=jnp.float32
        )
        return result_major + result_minor

    blended = lax.map(one_head, (place_heads, weight_heads, per_head))
    return jnp.transpose(blended, (1, 0, 2))


def body(
    features,
    corners,
    bilinear,
    attention,
    w_value,
    b_value,
    w_out,
    b_out,
    norm1_gain,
    norm1_bias,
    w_in,
    b_in,
    w_ffout,
    b_ffout,
    norm2_gain,
    norm2_bias,
):
    band_rows, model_width = features.shape
    samples = LEVELS * POINTS * 4
    segment_rows = [ROWS_DEV // 4**level_index for level_index in range(LEVELS)]
    segment_start = [sum(segment_rows[:level_index]) for level_index in range(LEVELS)]
    value_rows = (jnp.dot(features, w_value, preferred_element_type=jnp.float32) + b_value).astype(
        jnp.bfloat16
    )
    weight = (
        attention.reshape(band_rows, HEADS, LEVELS, POINTS, 1)
        * bilinear.reshape(band_rows, HEADS, LEVELS, POINTS, 4)
    ).astype(jnp.bfloat16)
    weight_heads = jnp.transpose(weight.reshape(band_rows, HEADS, samples), (1, 0, 2))
    corner_table = corners.reshape(band_rows, HEADS, LEVELS, POINTS * 4)
    places = []
    for level_index in range(LEVELS):
        level_corner = corner_table[:, :, level_index]
        places.append(
            level_corner // segment_rows[level_index] * band_rows
            + segment_start[level_index]
            + level_corner % segment_rows[level_index]
        )
    place_table = jnp.stack(places, axis=2).reshape(band_rows, HEADS, samples)
    place_heads = jnp.transpose(place_table, (1, 0, 2))
    whole = lax.all_gather(value_rows, "band", axis=0, tiled=True)
    running_sum = blend_rows(place_heads, weight_heads, whole)
    sampled = running_sum.reshape(band_rows, model_width).astype(jnp.bfloat16)
    attended = jnp.dot(sampled, w_out, preferred_element_type=jnp.float32) + b_out
    middle = layer_norm(features.astype(jnp.float32) + attended, norm1_gain, norm1_bias).astype(
        jnp.bfloat16
    )
    hidden = jnp.maximum(
        jnp.dot(middle, w_in, preferred_element_type=jnp.float32) + b_in, 0.0
    ).astype(jnp.bfloat16)
    result = (
        middle.astype(jnp.float32)
        + jnp.dot(hidden, w_ffout, preferred_element_type=jnp.float32)
        + b_ffout
    )
    return layer_norm(result, norm2_gain, norm2_bias).astype(jnp.bfloat16)


def solution(mesh):
    in_specs = (
        P(("dp", "band"), None),
        P(("dp", "band"), None),
        P(("dp", "band"), None),
        P(("dp", "band"), None),
        P(),
        P(),
        P(),
        P(),
        P(),
        P(),
        P(),
        P(),
        P(),
        P(),
        P(),
        P(),
    )
    out_specs = P(("dp", "band"), None)
    return jax.shard_map(body, mesh=mesh, in_specs=in_specs, out_specs=out_specs, check_vma=False)
```

profile of v0, /device:TPU:0, one launch (start us, length us, event | category | flops | bytes accessed | tf_op | source)
XLA Modules:
  0.0 79.4 jit_solution(4346520079388380277)
XLA Ops:
  0.0 1.3 %copy.37 = s32[255,512]{0,1:T(8,128)S(1)} copy(s32[255,512]{1,0:T(8,128)} %param.19) | data formatting | bytes 1044480 | tf_op args[1]
  1.3 0.5 fusion.32
  2.5 34.5 %all-gather = bf16[8,255,256]{2,1,0:T(8,128)(2,1)S(1)} all-gather(bf16[1,255,256]{2,1,0:T(8,128)(2,1)S(1)} %fusion.27), channel_id=1, replica_groups=mesh['dp'=4,'band'=8] {'band'}, dimensions={0}, use_global_device_ids=true | all-gather | bytes 1175040 | tf_op jit(solution)/shard_map/all_gather | solution.py:95
  37.3 0.7 copy.49
  38.4 0.8 copy-done.2
  40.0 36.1 %while.13 = (s32[]{:T(128)}, bf16[8,255,32]{1,2,0:T(8,128)(2,1)S(1)}, s32[8,255,64]{1,2,0:T(8,128)S(1)}, bf16[8,255,64]{1,0,2:T(8,128)(2,1)S(1)}, bf16[8,16,128,32]{2,1,3,0:T(8,128)(2,1)S(1)}, /*index=5*/s32[]{:T(128)}) while((s32[]{:T(128)}, bf16[8,255,32]{1,2,0:T(8,128)(2,1)S(1)}, s32[8,255,64]{1,2,0:T(8,128)S(1)}, ...), condition=%wide.region_1.2_spmd.clone, body=%wide.region_0.1_spmd.clone.sunk | while | flops 138711840 | bytes 5551189 | solution.py:50
  40.5 3.1 %subtract_convert_fusion.2 = (bf16[255,16,128]{2,1,0:T(8,128)(2,1)S(1)}, bf16[255,16,128]{2,1,0:T(8,128)(2,1)S(1)}) fusion(s32[255,64]{1,0:T(8,128)S(1)} %get-tuple-element.178, s32[255,64]{1,0:T(8,128)S(1)} %get-tuple-element.179, bf16[255,64]{1,0:T(8,128)(2,1)S(1)} %bitcast.93), kind=kOutput, calls=%fused_computation.6.clone.1 | convolution fusion | flops 71546880 | bytes 2252160 | tf_op jit(solution)/shard_map/while/body/eval_jaxpr/qsa,qsb->qab/dot_general | solution.py:37
  44.1 0.4 fusion.68
  45.0 3.1 %subtract_convert_fusion.2 = (bf16[255,16,128]{2,1,0:T(8,128)(2,1)S(1)}, bf16[255,16,128]{2,1,0:T(8,128)(2,1)S(1)}) fusion(s32[255,64]{1,0:T(8,128)S(1)} %get-tuple-element.178, s32[255,64]{1,0:T(8,128)S(1)} %get-tuple-element.179, bf16[255,64]{1,0:T(8,128)(2,1)S(1)} %bitcast.93), kind=kOutput, calls=%fused_computation.6.clone.1 | convolution fusion | flops 71546880 | bytes 2252160 | tf_op jit(solution)/shard_map/while/body/eval_jaxpr/qsa,qsb->qab/dot_general | solution.py:37
  48.6 0.4 fusion.68
  49.5 3.1 %subtract_convert_fusion.2 = (bf16[255,16,128]{2,1,0:T(8,128)(2,1)S(1)}, bf16[255,16,128]{2,1,0:T(8,128)(2,1)S(1)}) fusion(s32[255,64]{1,0:T(8,128)S(1)} %get-tuple-element.178, s32[255,64]{1,0:T(8,128)S(1)} %get-tuple-element.179, bf16[255,64]{1,0:T(8,128)(2,1)S(1)} %bitcast.93), kind=kOutput, calls=%fused_computation.6.clone.1 | convolution fusion | flops 71546880 | bytes 2252160 | tf_op jit(solution)/shard_map/while/body/eval_jaxpr/qsa,qsb->qab/dot_general | solution.py:37
  53.1 0.4 fusion.68
  54.0 3.1 %subtract_convert_fusion.2 = (bf16[255,16,128]{2,1,0:T(8,128)(2,1)S(1)}, bf16[255,16,128]{2,1,0:T(8,128)(2,1)S(1)}) fusion(s32[255,64]{1,0:T(8,128)S(1)} %get-tuple-element.178, s32[255,64]{1,0:T(8,128)S(1)} %get-tuple-element.179, bf16[255,64]{1,0:T(8,128)(2,1)S(1)} %bitcast.93), kind=kOutput, calls=%fused_computation.6.clone.1 | convolution fusion | flops 71546880 | bytes 2252160 | tf_op jit(solution)/shard_map/while/body/eval_jaxpr/qsa,qsb->qab/dot_general | solution.py:37
  57.6 0.4 fusion.68
  58.5 3.1 %subtract_convert_fusion.2 = (bf16[255,16,128]{2,1,0:T(8,128)(2,1)S(1)}, bf16[255,16,128]{2,1,0:T(8,128)(2,1)S(1)}) fusion(s32[255,64]{1,0:T(8,128)S(1)} %get-tuple-element.178, s32[255,64]{1,0:T(8,128)S(1)} %get-tuple-element.179, bf16[255,64]{1,0:T(8,128)(2,1)S(1)} %bitcast.93), kind=kOutput, calls=%fused_computation.6.clone.1 | convolution fusion | flops 71546880 | bytes 2252160 | tf_op jit(solution)/shard_map/while/body/eval_jaxpr/qsa,qsb->qab/dot_general | solution.py:37
  62.1 0.4 fusion.68
  63.0 3.1 %subtract_convert_fusion.2 = (bf16[255,16,128]{2,1,0:T(8,128)(2,1)S(1)}, bf16[255,16,128]{2,1,0:T(8,128)(2,1)S(1)}) fusion(s32[255,64]{1,0:T(8,128)S(1)} %get-tuple-element.178, s32[255,64]{1,0:T(8,128)S(1)} %get-tuple-element.179, bf16[255,64]{1,0:T(8,128)(2,1)S(1)} %bitcast.93), kind=kOutput, calls=%fused_computation.6.clone.1 | convolution fusion | flops 71546880 | bytes 2252160 | tf_op jit(solution)/shard_map/while/body/eval_jaxpr/qsa,qsb->qab/dot_general | solution.py:37
  66.6 0.4 fusion.68
  67.5 3.1 %subtract_convert_fusion.2 = (bf16[255,16,128]{2,1,0:T(8,128)(2,1)S(1)}, bf16[255,16,128]{2,1,0:T(8,128)(2,1)S(1)}) fusion(s32[255,64]{1,0:T(8,128)S(1)} %get-tuple-element.178, s32[255,64]{1,0:T(8,128)S(1)} %get-tuple-element.179, bf16[255,64]{1,0:T(8,128)(2,1)S(1)} %bitcast.93), kind=kOutput, calls=%fused_computation.6.clone.1 | convolution fusion | flops 71546880 | bytes 2252160 | tf_op jit(solution)/shard_map/while/body/eval_jaxpr/qsa,qsb->qab/dot_general | solution.py:37
  71.1 0.4 fusion.68
  72.0 3.1 %subtract_convert_fusion.2 = (bf16[255,16,128]{2,1,0:T(8,128)(2,1)S(1)}, bf16[255,16,128]{2,1,0:T(8,128)(2,1)S(1)}) fusion(s32[255,64]{1,0:T(8,128)S(1)} %get-tuple-element.178, s32[255,64]{1,0:T(8,128)S(1)} %get-tuple-element.179, bf16[255,64]{1,0:T(8,128)(2,1)S(1)} %bitcast.93), kind=kOutput, calls=%fused_computation.6.clone.1 | convolution fusion | flops 71546880 | bytes 2252160 | tf_op jit(solution)/shard_map/while/body/eval_jaxpr/qsa,qsb->qab/dot_general | solution.py:37
  75.6 0.4 fusion.68
  76.7 1.7 %fusion.56 = (f32[255]{0:T(256)S(1)}, f32[255,256]{1,0:T(8,128)S(1)}) fusion(f32[256]{0:T(256)S(1)} %copy-done.11, bf16[1024,256]{1,0:T(8,128)(2,1)S(1)} %copy-done, bf16[256,1024]{1,0:T(8,128)(2,1)} %param.28, f32[1024]{0:T(1024)S(1)} %copy-done.10, f32[255,256]{1,0:T(8,128)S(1)} %get-tuple-element.140, f32[256]{0:T(256)S(1)} %copy-done.12, ...), kind=kOutput, calls=%fused_computation.95 | convolution fusion | flops 269083904 | bytes 1581044 | tf_op jit(solution)/shard_map/dot_general | solution.py:107
  78.6 0.8 %add_convert_fusion = bf16[255,256]{1,0:T(8,128)(2,1)} fusion(f32[255,256]{1,0:T(8,128)S(1)} %get-tuple-element.142, f32[256]{0:T(256)S(1)} %copy-done.8, f32[256]{0:T(256)S(1)} %copy-done.9, f32[255]{0:T(256)S(1)} %add_rsqrt_fusion, f32[255]{0:T(256)S(1)} %broadcast_multiply_fusion), kind=kLoop, calls=%fused_computation.50 | loop fusion | flops 326400 | bytes 395768 | tf_op jit(solution)/shard_map/convert_element_type | solution.py:110
  (101 shorter events, 9.6 us)
Async XLA Ops:
  0.0 76.6 %copy-start = (bf16[1024,256]{1,0:T(8,128)(2,1)S(1)}, bf16[1024,256]{1,0:T(8,128)(2,1)}, u32[]{:S(2)}) copy-start(bf16[1024,256]{1,0:T(8,128)(2,1)} %param.30) | copy-start | bytes 1572868
  1.3 0.9 %copy-start.1 = (bf16[255,256]{1,0:T(8,128)(2,1)S(1)}, bf16[255,256]{1,0:T(8,128)(2,1)}, u32[]{:S(2)}) copy-start(bf16[255,256]{1,0:T(8,128)(2,1)} %param.18) | copy-start | bytes 391684
  1.3 1.0 %copy-start.3 = (bf16[256,256]{1,0:T(8,128)(2,1)S(1)}, bf16[256,256]{1,0:T(8,128)(2,1)}, u32[]{:S(2)}) copy-start(bf16[256,256]{1,0:T(8,128)(2,1)} %param.22) | copy-start | bytes 393220
  1.3 1.0 %copy-start.6 = (f32[256]{0:T(256)S(1)}, f32[256]{0:T(256)}, u32[]{:S(2)}) copy-start(f32[256]{0:T(256)} %param.23) | copy-start | bytes 3076
  38.1 1.0 %copy-start.2 = (f32[255,512]{1,0:T(8,128)S(1)}, f32[255,512]{1,0:T(8,128)}, u32[]{:S(2)}) copy-start(f32[255,512]{1,0:T(8,128)} %param.20) | copy-start | bytes 1566724
  38.4 1.0 %copy-start.5 = (f32[255,128]{1,0:T(8,128)S(1)}, f32[255,128]{1,0:T(8,128)}, u32[]{:S(2)}) copy-start(f32[255,128]{1,0:T(8,128)} %param.21) | copy-start | bytes 391684
  39.9 36.1 %copy-start.4 = (bf16[256,256]{1,0:T(8,128)(2,1)S(1)}, bf16[256,256]{1,0:T(8,128)(2,1)}, u32[]{:S(2)}) copy-start(bf16[256,256]{1,0:T(8,128)(2,1)} %param.24) | copy-start | bytes 393220
  39.9 36.1 %copy-start.7 = (f32[256]{0:T(256)S(1)}, f32[256]{0:T(256)}, u32[]{:S(2)}) copy-start(f32[256]{0:T(256)} %param.25) | copy-start | bytes 3076
  40.0 36.7 %copy-start.10 = (f32[1024]{0:T(1024)S(1)}, f32[1024]{0:T(1024)}, u32[]{:S(2)}) copy-start(f32[1024]{0:T(1024)} %param.29) | copy-start | bytes 12292
  40.0 36.7 %copy-start.11 = (f32[256]{0:T(256)S(1)}, f32[256]{0:T(256)}, u32[]{:S(2)}) copy-start(f32[256]{0:T(256)} %param.31) | copy-start | bytes 3076
  40.0 36.7 %copy-start.12 = (f32[256]{0:T(256)S(1)}, f32[256]{0:T(256)}, u32[]{:S(2)}) copy-start(f32[256]{0:T(256)} %param.27) | copy-start | bytes 3076
  40.0 36.7 %copy-start.13 = (f32[256]{0:T(256)S(1)}, f32[256]{0:T(256)}, u32[]{:S(2)}) copy-start(f32[256]{0:T(256)} %param.26) | copy-start | bytes 3076
  76.7 2.0 %copy-start.8 = (f32[256]{0:T(256)S(1)}, f32[256]{0:T(256)}, u32[]{:S(2)}) copy-start(f32[256]{0:T(256)} %param.33) | copy-start | bytes 3076
  76.7 1.9 %copy-start.9 = (f32[256]{0:T(256)S(1)}, f32[256]{0:T(256)}, u32[]{:S(2)}) copy-start(f32[256]{0:T(256)} %param.32) | copy-start | bytes 3076
where the time goes:
time: 79.6 us; the launch traced here: 79.4 us
  blocking collectives  34.5 us (43%)
  matrix products  34.2 us (43%)
  local copies, waits for them, and re-layouts  6.87 us (9%)
  other arithmetic  3.03 us (4%)
    all_gather x1, blocking collectives, body(): whole = lax.all_gather(value_rows, 'band', axis=0, tiled=True)  34.5 us
    dot_general x8, matrix products, one_head(): jnp.einsum('qsa,qsb->qab', group_hits, lane_hits, preferred_element_type=...  25.1 us
    unnamed x35, local copies, waits for them, and re-layouts  4.12 us
    dot_general x8, matrix products, one_head(): jnp.einsum('qab,abd->qd', table_minor, value_one, preferred_element_type=...  3.53 us
    dot_general x8, matrix products, one_head(): jnp.einsum('qab,abd->qd', table_major, value_one, preferred_element_type=...  3.31 us
    dynamic_slice x40, local copies, waits for them, and re-layouts, blend_rows(): blended = lax.map(one_head, (place_heads, weight_heads, per_head))  2.63 us
    dot_general x1, matrix products, body(): jnp.dot(hidden, w_ffout, preferred_element_type=jnp.float32)  1.72 us

commit v1 on v0

v1 whole, which is shorter than its diff:
```python
import functools

import jax
import jax.numpy as jnp
from jax import lax
from jax.experimental import pallas as pl
from jax.experimental.pallas import tpu as pltpu
from jax.sharding import PartitionSpec as P

HEADS = 8
LEVELS = 4
POINTS = 4
ROWS_DEV = 192
MAP_W = 128
LANES = 128
STRIDE = LANES - 1

F32 = jnp.float32
BF16 = jnp.bfloat16
MESH = pl.DeviceIdType.MESH


def plan(bands):
    rows = [ROWS_DEV // 4**level for level in range(LEVELS)]
    starts = [sum(rows[:level]) for level in range(LEVELS)]
    widths = [MAP_W // 2**level for level in range(LEVELS)]
    lengths = [count * bands for count in rows]
    merged, used = {}, 0
    for level in reversed(range(LEVELS)):
        if used + lengths[level] <= LANES:
            merged[level] = used
            used += lengths[level]
        else:
            break
    windowed = [level for level in range(LEVELS) if level not in merged]
    groups = {level: (lengths[level] - widths[level] - 2) // STRIDE + 1 for level in windowed}
    return rows, starts, widths, lengths, merged, windowed, groups


def flat_lanes(length, width, groups):
    need = STRIDE * (groups - 1) + width + LANES
    return -(-max(length, need) // LANES) * LANES


def norm(inputs, gain, shift):
    average = jnp.mean(inputs, axis=-1, keepdims=True)
    centred = inputs - average
    variance = jnp.mean(centred * centred, axis=-1, keepdims=True)
    return centred * lax.rsqrt(variance + 1e-05) * gain + shift


def one_hot_pair(iota, place, weights):
    low = iota == place
    high = iota == place + 1.0
    zero = jnp.zeros((), F32)
    top = jnp.where(low, weights[0], jnp.where(high, weights[1], zero))
    bottom = jnp.where(low, weights[2], jnp.where(high, weights[3], zero))
    return top, bottom


def kernel(
    bands,
    feat,
    corners,
    bilinear,
    attention,
    w_value,
    b_value,
    w_out_hbm,
    b_out,
    gain1,
    bias1,
    w_in_hbm,
    b_in,
    w_ff_hbm,
    b_ff,
    gain2,
    bias2,
    out,
    gathered,
    place_t,
    group_t,
    bil_t,
    att_t,
    hot,
    hot_merged,
    table_merged,
    samp_t,
    w_out,
    w_in,
    w_ff,
    send_sem,
    recv_sem,
    load_sem,
    *level_scratch,
):
    rows, starts, widths, lengths, merged, windowed, groups = plan(bands)
    flats = level_scratch[:LEVELS]
    tables = dict(zip(windowed, level_scratch[LEVELS:]))
    tokens, model = feat.shape
    head_dim = model // HEADS
    padded = place_t.shape[1]
    me = lax.axis_index("band")

    loads = [
        pltpu.make_async_copy(source, target, load_sem.at[number])
        for number, (source, target) in enumerate(
            ((w_out_hbm, w_out), (w_in_hbm, w_in), (w_ff_hbm, w_ff))
        )
    ]
    for load in loads:
        load.start()

    barrier = pltpu.get_barrier_semaphore()
    for offset in range(1, bands):
        pl.semaphore_signal(
            barrier, inc=1, device_id={"band": lax.rem(me + offset, bands)}, device_id_type=MESH
        )
    pl.semaphore_wait(barrier, bands - 1)

    def send(offset):
        return pltpu.make_async_remote_copy(
            src_ref=feat,
            dst_ref=gathered.at[me],
            send_sem=send_sem.at[offset],
            recv_sem=recv_sem.at[me],
            device_id={"band": lax.rem(me + offset, bands)},
            device_id_type=MESH,
        )

    for offset in range(1, bands):
        send(offset).start()

    gathered[me] = feat[...]

    def turned(block):
        tail = jnp.zeros((padded - tokens, block.shape[1]), F32)
        return jnp.transpose(jnp.concatenate([block, tail], axis=0))

    corner_t = turned(corners[...].astype(F32))
    group_t[...] = jnp.floor((corner_t + 0.5) * (1.0 / STRIDE))
    place_t[...] = corner_t
    bil_t[...] = turned(bilinear[...])
    att_t[...] = turned(attention[...])
    for level in range(LEVELS):
        flats[level][...] = jnp.zeros(flats[level].shape, F32)

    iota = lax.broadcasted_iota(jnp.int32, (LANES, padded), 0).astype(F32)

    def point_weights(point):
        share = att_t[pl.ds(point, 1), :]
        return [
            (share * bil_t[pl.ds(point * 4 + corner, 1), :]).astype(BF16).astype(F32)
            for corner in range(4)
        ]

    def build(head, carry):
        for slot, level in enumerate(windowed):
            for which in range(POINTS):
                point = (head * LEVELS + level) * POINTS + which
                place = place_t[pl.ds(point * 4, 1), :] - STRIDE * group_t[pl.ds(point * 4, 1), :]
                top, bottom = one_hot_pair(iota, place, point_weights(point))
                hot[head, slot * POINTS + which, 0:LANES, :] = top.astype(BF16)
                hot[head, slot * POINTS + which, LANES:, :] = bottom.astype(BF16)
        top_sum = jnp.zeros((LANES, padded), F32)
        bottom_sum = jnp.zeros((LANES, padded), F32)
        for level in merged:
            for which in range(POINTS):
                point = (head * LEVELS + level) * POINTS + which
                place = place_t[pl.ds(point * 4, 1), :] + float(merged[level])
                top, bottom = one_hot_pair(iota, place, point_weights(point))
                top_sum += top
                bottom_sum += bottom
        hot_merged[head, 0:LANES, :] = top_sum.astype(BF16)
        hot_merged[head, LANES:, :] = bottom_sum.astype(BF16)
        return carry

    lax.fori_loop(0, HEADS, build, 0)

    w_value_t = jnp.transpose(w_value[...].astype(F32)).astype(BF16)
    shift_t = jnp.transpose(jnp.broadcast_to(b_value[...], (LANES, model)))[:, 0:1]

    for offset in range(1, bands):
        copy = pltpu.make_async_remote_copy(
            src_ref=feat,
            dst_ref=gathered.at[lax.rem(me - offset + bands, bands)],
            send_sem=send_sem.at[offset],
            recv_sem=recv_sem.at[lax.rem(me - offset + bands, bands)],
            device_id={"band": lax.rem(me + offset, bands)},
            device_id_type=MESH,
        )
        copy.wait_recv()

    for band in range(bands):
        value_t = lax.dot_general(
            w_value_t, gathered[band], (((1,), (1,)), ((), ())), preferred_element_type=F32
        )
        value_t = (value_t + shift_t).astype(BF16).astype(F32)
        for level in range(LEVELS):
            count = rows[level]
            flats[level][:, band * count : (band + 1) * count] = value_t[
                :, starts[level] : starts[level] + count
            ]

    for level in windowed:
        for group in range(groups[level]):
            base = STRIDE * group
            top = flats[level][:, base : base + LANES].astype(BF16)
            under = base + widths[level]
            bottom = flats[level][:, under : under + LANES].astype(BF16)
            for head in range(HEADS):
                part = slice(head * head_dim, (head + 1) * head_dim)
                into = slice(group * head_dim, (group + 1) * head_dim)
                tables[level][head, into, 0:LANES] = top[part, :]
                tables[level][head, into, LANES:] = bottom[part, :]
    lane = lax.broadcasted_iota(jnp.int32, (1, LANES), 1)
    top = jnp.zeros((model, LANES), F32)
    bottom = jnp.zeros((model, LANES), F32)
    for level, begin in merged.items():
        inside = (lane >= begin) & (lane < begin + lengths[level])
        piece = flats[level][:, 0:LANES]
        top += jnp.where(inside, pltpu.roll(piece, begin, 1), 0.0)
        bottom += jnp.where(
            inside, pltpu.roll(piece, (begin - widths[level]) % LANES, 1), 0.0
        )
    for head in range(HEADS):
        part = slice(head * head_dim, (head + 1) * head_dim)
        table_merged[head, :, 0:LANES] = top[part, :].astype(BF16)
        table_merged[head, :, LANES:] = bottom[part, :].astype(BF16)

    def blend(head, carry):
        total = jnp.dot(table_merged[head], hot_merged[head], preferred_element_type=F32)
        for slot, level in enumerate(windowed):
            for which in range(POINTS):
                point = (head * LEVELS + level) * POINTS + which
                mine = group_t[pl.ds(point * 4, 1), :]
                picked = jnp.dot(
                    tables[level][head],
                    hot[head, slot * POINTS + which],
                    preferred_element_type=F32,
                )
                for group in range(groups[level]):
                    total += jnp.where(
                        mine == float(group),
                        picked[group * head_dim : (group + 1) * head_dim, :],
                        0.0,
                    )
        samp_t[pl.ds(pl.multiple_of(head * head_dim, head_dim), head_dim), :] = total
        return carry

    lax.fori_loop(0, HEADS, blend, 0)

    for load in loads:
        load.wait()
    sampled = jnp.transpose(samp_t[...])[0:tokens, :].astype(BF16)
    attended = jnp.dot(sampled, w_out[...], preferred_element_type=F32) + b_out[...]
    middle = norm(feat[...].astype(F32) + attended, gain1[...], bias1[...]).astype(BF16)
    hidden = jnp.maximum(
        jnp.dot(middle, w_in[...], preferred_element_type=F32) + b_in[...], 0.0
    ).astype(BF16)
    result = (
        middle.astype(F32)
        + jnp.dot(hidden, w_ff[...], preferred_element_type=F32)
        + b_ff[...]
    )
    out[...] = norm(result, gain2[...], bias2[...]).astype(BF16)
    for offset in range(1, bands):
        send(offset).wait_send()


def body(bands, *args):
    feat, corners = args[0], args[1]
    tokens, model = feat.shape
    padded = -(-tokens // LANES) * LANES
    rows, starts, widths, lengths, merged, windowed, groups = plan(bands)
    head_dim = model // HEADS
    samples = corners.shape[1]
    operands = [
        argument.reshape(1, -1) if argument.ndim == 1 else argument for argument in args
    ]
    anywhere = {6, 10, 12}
    specs = [
        pl.BlockSpec(memory_space=pl.ANY if number in anywhere else pltpu.VMEM)
        for number in range(len(operands))
    ]
    flat_shapes = [
        pltpu.VMEM(
            (model, flat_lanes(lengths[level], widths[level], groups.get(level, 1))), F32
        )
        for level in range(LEVELS)
    ]
    table_shapes = [
        pltpu.VMEM((HEADS, groups[level] * head_dim, 2 * LANES), BF16) for level in windowed
    ]
    scratch = [
        pltpu.VMEM((bands, tokens, model), BF16),
        pltpu.VMEM((samples, padded), F32),
        pltpu.VMEM((samples, padded), F32),
        pltpu.VMEM((samples, padded), F32),
        pltpu.VMEM((samples // 4, padded), F32),
        pltpu.VMEM((HEADS, len(windowed) * POINTS, 2 * LANES, padded), BF16),
        pltpu.VMEM((HEADS, 2 * LANES, padded), BF16),
        pltpu.VMEM((HEADS, head_dim, 2 * LANES), BF16),
        pltpu.VMEM((model, padded), F32),
        pltpu.VMEM(args[6].shape, BF16),
        pltpu.VMEM(args[10].shape, BF16),
        pltpu.VMEM(args[12].shape, BF16),
        pltpu.SemaphoreType.DMA((bands,)),
        pltpu.SemaphoreType.DMA((bands,)),
        pltpu.SemaphoreType.DMA((3,)),
    ] + flat_shapes + table_shapes
    return pl.pallas_call(
        functools.partial(kernel, bands),
        out_shape=jax.ShapeDtypeStruct((tokens, model), BF16),
        in_specs=specs,
        out_specs=pl.BlockSpec(memory_space=pltpu.VMEM),
        scratch_shapes=scratch,
        compiler_params=pltpu.CompilerParams(
            collective_id=0, has_side_effects=True, vmem_limit_bytes=60 * 1024 * 1024
        ),
        name="layer",
    )(*operands)


def solution(mesh):
    split = P(("dp", "band"), None)
    in_specs = (split,) * 4 + (P(),) * 12
    return jax.shard_map(
        functools.partial(body, mesh.shape["band"]),
        mesh=mesh,
        in_specs=in_specs,
        out_specs=split,
        check_vma=False,
    )
```

time: 79.6 us -> 37.7 us (0.47)
  the two profiles are of different devices: /device:TPU:0 before, /device:TPU:15 now
where the time goes in v1:
time: 37.7 us; the launch traced here: 37.6 us
  Pallas kernels  36 us (95%)
  local copies, waits for them, and re-layouts  1.57 us (4%)
    pallas_call x1, Pallas kernels, body(): pl.pallas_call(functools.partial(kernel, bands), out_shape=jax.ShapeDtype...  36 us
    unnamed x1, local copies, waits for them, and re-layouts  1.57 us

profile of v1, /device:TPU:15, one launch (start us, length us, event | category | flops | bytes accessed | tf_op | source)
XLA Modules:
  0.0 37.6 jit_solution(13243816297441219945)
XLA Ops:
  0.0 36.0 %layer.1 = bf16[255,256]{1,0:T(8,128)(2,1)} custom-call(bf16[255,256]{1,0:T(8,128)(2,1)} %feat.1, s32[255,512]{1,0:T(8,128)} %corners.1, f32[255,512]{1,0:T(8,128)} %bilinear.1, f32[255,128]{1,0:T(8,128)} %attention.1, bf16[256,256]{1,0:T(8,128)(2,1)} %w_value.1, f32[1,256]{1,0:T(1,128)} %bitcast.9, bf16[256,256]{1,0:T(8,128)(2,1)} %w_out_hbm.1, ...), custom_call_target="tpu_custom_call" | custom-call | tf_op jit(solution)/shard_map/layer/pallas_call | solution.py:312
  36.0 1.6 %copy.18 = bf16[255,256]{1,0:T(8,128)(2,1)} copy(bf16[255,256]{1,0:T(8,128)(2,1)} %layer.1) | data formatting | bytes 261120

commit v2 on v1

--- a/solution.py
+++ b/solution.py
@@ -14,6 +14,8 @@
 MAP_W = 128
 LANES = 128
 STRIDE = LANES - 1
+CHUNK = 128
+BUILT = (3, 5, 7, 8)
 
 F32 = jnp.float32
 BF16 = jnp.bfloat16
@@ -61,10 +63,10 @@
 def kernel(
     bands,
     feat,
-    corners,
-    bilinear,
-    attention,
-    w_value,
+    corners_hbm,
+    bilinear_hbm,
+    attention_hbm,
+    w_value_hbm,
     b_value,
     w_out_hbm,
     b_out,
@@ -78,6 +80,13 @@
     bias2,
     out,
     gathered,
+    values,
+    corners,
+    bilinear,
+    attention,
+    w_value,
+    w_value_t,
+    shift_t,
     place_t,
     group_t,
     bil_t,
@@ -102,36 +111,102 @@
     padded = place_t.shape[1]
     me = lax.axis_index("band")
 
+    line = bands // 2
+    mine_z, mine_y = me // 2, lax.rem(me, 2)
+    partner = mine_z * 2 + 1 - mine_y
+    has_left, has_right = mine_z > 0, mine_z < line - 1
+    cuts = [(begin, min(begin + CHUNK, tokens) - begin) for begin in range(0, tokens, CHUNK)]
+
+    sources = (corners_hbm, bilinear_hbm, attention_hbm, w_value_hbm, w_out_hbm, w_in_hbm, w_ff_hbm)
+    targets = (corners, bilinear, attention, w_value, w_out, w_in, w_ff)
     loads = [
         pltpu.make_async_copy(source, target, load_sem.at[number])
-        for number, (source, target) in enumerate(
-            ((w_out_hbm, w_out), (w_in_hbm, w_in), (w_ff_hbm, w_ff))
-        )
+        for number, (source, target) in enumerate(zip(sources, targets))
     ]
+
+    barrier = pltpu.get_barrier_semaphore()
+
+    def greet(target):
+        pl.semaphore_signal(barrier, inc=1, device_id={"band": target}, device_id_type=MESH)
+
+    greet(partner)
+    pl.when(has_left)(lambda: greet(me - 2))
+    pl.when(has_right)(lambda: greet(me + 2))
+    pl.semaphore_wait(
+        barrier, 1 + has_left.astype(jnp.int32) + has_right.astype(jnp.int32)
+    )
+
+    def copy_of(source, block, cut, target, lane):
+        begin, count = cuts[cut]
+        return pltpu.make_async_remote_copy(
+            src_ref=source.at[pl.ds(begin, count)],
+            dst_ref=gathered.at[block, pl.ds(begin, count)],
+            send_sem=send_sem.at[lane, block, cut],
+            recv_sem=recv_sem.at[block, cut],
+            device_id={"band": target},
+            device_id_type=MESH,
+        )
+
+    def moves(block, cut, source=None):
+        source = gathered.at[block] if source is None else source
+        left = copy_of(source, block, cut, me - 2, 0)
+        right = copy_of(source, block, cut, me + 2, 1)
+        across = copy_of(source, block, cut, partner, 2)
+        return left, right, across
+
+    for cut in range(len(cuts)):
+        left, right, across = moves(me, cut, feat)
+        pl.when(has_left)(left.start)
+        pl.when(has_right)(right.start)
+        across.start()
     for load in loads:
         load.start()
 
-    barrier = pltpu.get_barrier_semaphore()
-    for offset in range(1, bands):
-        pl.semaphore_signal(
-            barrier, inc=1, device_id={"band": lax.rem(me + offset, bands)}, device_id_type=MESH
-        )
-    pl.semaphore_wait(barrier, bands - 1)
-
-    def send(offset):
-        return pltpu.make_async_remote_copy(
-            src_ref=feat,
-            dst_ref=gathered.at[me],
-            send_sem=send_sem.at[offset],
-            recv_sem=recv_sem.at[me],
-            device_id={"band": lax.rem(me + offset, bands)},
-            device_id_type=MESH,
-        )
-
-    for offset in range(1, bands):
-        send(offset).start()
-
-    gathered[me] = feat[...]
+    def project(rows_in, block):
+        value_t = lax.dot_general(
+            w_value_t[...], rows_in, (((1,), (1,)), ((), ())), preferred_element_type=F32
+        )
+        values[block, :, 0:tokens] = (value_t + shift_t[:, 0:1]).astype(BF16).astype(F32)
+
+    def stage(distance, cut):
+        before, after = me - 2 * distance, me + 2 * distance
+
+        @pl.when(mine_z >= distance)
+        def _():
+            left, right, across = moves(before, cut)
+            across.wait_recv()
+            pl.when(has_right)(right.start)
+            across.start()
+
+        @pl.when(mine_z + distance < line)
+        def _():
+            left, right, across = moves(after, cut)
+            across.wait_recv()
+            pl.when(has_left)(left.start)
+            across.start()
+
+        if cut == len(cuts) - 1:
+            pl.when(mine_z >= distance)(lambda: project(gathered[before], before))
+            pl.when(mine_z + distance < line)(lambda: project(gathered[after], after))
+
+    def arrive(block):
+        for cut in range(len(cuts)):
+            moves(block, cut)[2].wait_recv()
+        project(gathered[block], block)
+
+    def finish(block, came_left, came_right, own=False):
+        for cut in range(len(cuts)):
+            left, right, across = moves(block, cut, feat if own else None)
+            if own or came_right:
+                pl.when(has_left)(left.wait_send)
+            if own or came_left:
+                pl.when(has_right)(right.wait_send)
+            across.wait_send()
+
+    for load in loads[:4]:
+        load.wait()
+    w_value_t[...] = jnp.transpose(w_value[...].astype(F32)).astype(BF16)
+    shift_t[...] = jnp.transpose(jnp.broadcast_to(b_value[...], (LANES, model)))
 
     def turned(block):
         tail = jnp.zeros((padded - tokens, block.shape[1]), F32)
@@ -175,27 +250,25 @@
         hot_merged[head, LANES:, :] = bottom_sum.astype(BF16)
         return carry
 
-    lax.fori_loop(0, HEADS, build, 0)
-
-    w_value_t = jnp.transpose(w_value[...].astype(F32)).astype(BF16)
-    shift_t = jnp.transpose(jnp.broadcast_to(b_value[...], (LANES, model)))[:, 0:1]
-
-    for offset in range(1, bands):
-        copy = pltpu.make_async_remote_copy(
-            src_ref=feat,
-            dst_ref=gathered.at[lax.rem(me - offset + bands, bands)],
-            send_sem=send_sem.at[offset],
-            recv_sem=recv_sem.at[lax.rem(me - offset + bands, bands)],
-            device_id={"band": lax.rem(me + offset, bands)},
-            device_id_type=MESH,
-        )
-        copy.wait_recv()
+    stages = [(distance, cut) for distance in range(1, line) for cut in range(len(cuts))]
+    done = 0
+    for number, entry in enumerate(stages):
+        upto = min(HEADS, BUILT[min(number, len(BUILT) - 1)])
+        if upto > done:
+            lax.fori_loop(done, upto, build, 0)
+            done = upto
+        if number == 0:
+            project(feat[...], me)
+        stage(*entry)
+    if done < HEADS:
+        lax.fori_loop(done, HEADS, build, 0)
+    arrive(partner)
+    for distance in range(1, line):
+        pl.when(mine_z >= distance)(functools.partial(arrive, partner - 2 * distance))
+        pl.when(mine_z + distance < line)(functools.partial(arrive, partner + 2 * distance))
 
     for band in range(bands):
-        value_t = lax.dot_general(
-            w_value_t, gathered[band], (((1,), (1,)), ((), ())), preferred_element_type=F32
-        )
-        value_t = (value_t + shift_t).astype(BF16).astype(F32)
+        value_t = values[band]
         for level in range(LEVELS):
             count = rows[level]
             flats[level][:, band * count : (band + 1) * count] = value_t[
@@ -250,7 +323,7 @@
 
     lax.fori_loop(0, HEADS, blend, 0)
 
-    for load in loads:
+    for load in loads[4:]:
         load.wait()
     sampled = jnp.transpose(samp_t[...])[0:tokens, :].astype(BF16)
     attended = jnp.dot(sampled, w_out[...], preferred_element_type=F32) + b_out[...]
@@ -264,8 +337,14 @@
         + b_ff[...]
     )
     out[...] = norm(result, gain2[...], bias2[...]).astype(BF16)
-    for offset in range(1, bands):
-        send(offset).wait_send()
+    finish(me, False, False, own=True)
+    for distance in range(1, line):
+        pl.when(mine_z >= distance)(
+            functools.partial(finish, me - 2 * distance, True, False)
+        )
+        pl.when(mine_z + distance < line)(
+            functools.partial(finish, me + 2 * distance, False, True)
+        )
 
 
 def body(bands, *args):
@@ -278,7 +357,8 @@
     operands = [
         argument.reshape(1, -1) if argument.ndim == 1 else argument for argument in args
     ]
-    anywhere = {6, 10, 12}
+    anywhere = {1, 2, 3, 4, 6, 10, 12}
+    cuts = -(-tokens // CHUNK)
     specs = [
         pl.BlockSpec(memory_space=pl.ANY if number in anywhere else pltpu.VMEM)
         for number in range(len(operands))
@@ -294,6 +374,13 @@
     ]
     scratch = [
         pltpu.VMEM((bands, tokens, model), BF16),
+        pltpu.VMEM((bands, model, padded), F32),
+        pltpu.VMEM(args[1].shape, jnp.int32),
+        pltpu.VMEM(args[2].shape, F32),
+        pltpu.VMEM(args[3].shape, F32),
+        pltpu.VMEM(args[4].shape, BF16),
+        pltpu.VMEM(args[4].shape, BF16),
+        pltpu.VMEM((model, LANES), F32),
         pltpu.VMEM((samples, padded), F32),
         pltpu.VMEM((samples, padded), F32),
         pltpu.VMEM((samples, padded), F32),
@@ -305,9 +392,9 @@
         pltpu.VMEM(args[6].shape, BF16),
         pltpu.VMEM(args[10].shape, BF16),
         pltpu.VMEM(args[12].shape, BF16),
-        pltpu.SemaphoreType.DMA((bands,)),
-        pltpu.SemaphoreType.DMA((bands,)),
-        pltpu.SemaphoreType.DMA((3,)),
+        pltpu.SemaphoreType.DMA((3, bands, cuts)),
+        pltpu.SemaphoreType.DMA((bands, cuts)),
+        pltpu.SemaphoreType.DMA((len(anywhere),)),
     ] + flat_shapes + table_shapes
     return pl.pallas_call(
         functools.partial(kernel, bands),

time: 37.7 us -> 31.4 us (0.83)
  the two profiles are of different devices: /device:TPU:15 before, /device:TPU:0 now
where the time goes in v2:
time: 31.4 us; the launch traced here: 31.2 us
  Pallas kernels  29.7 us (95%)
  local copies, waits for them, and re-layouts  1.57 us (5%)
    pallas_call x1, Pallas kernels, body(): pl.pallas_call(functools.partial(kernel, bands), out_shape=jax.ShapeDtype...  29.7 us
    unnamed x1, local copies, waits for them, and re-layouts  1.57 us

profile of v2, /device:TPU:0, one launch (start us, length us, event | category | flops | bytes accessed | tf_op | source)
XLA Modules:
  0.0 31.2 jit_solution(14436328508894404972)
XLA Ops:
  0.0 29.7 %layer.1 = bf16[255,256]{1,0:T(8,128)(2,1)} custom-call(bf16[255,256]{1,0:T(8,128)(2,1)} %feat.1, s32[255,512]{1,0:T(8,128)} %corners_hbm.1, f32[255,512]{1,0:T(8,128)} %bilinear_hbm.1, f32[255,128]{1,0:T(8,128)} %attention_hbm.1, bf16[256,256]{1,0:T(8,128)(2,1)} %w_value_hbm.1, f32[1,256]{1,0:T(1,128)} %bitcast.9, bf16[256,256]{1,0:T(8,128)(2,1)} %w_out_hbm.1, ...), custom_call_target="tpu_custom_call" | custom-call | tf_op jit(solution)/shard_map/layer/pallas_call | solution.py:399
  29.7 1.6 %copy.18 = bf16[255,256]{1,0:T(8,128)(2,1)} copy(bf16[255,256]{1,0:T(8,128)(2,1)} %layer.1) | data formatting | bytes 261120

commit v3 on v2

--- a/solution.py
+++ b/solution.py
@@ -1,4 +1,5 @@
 import functools
+import math
 
 import jax
 import jax.numpy as jnp
@@ -14,8 +15,8 @@
 MAP_W = 128
 LANES = 128
 STRIDE = LANES - 1
-CHUNK = 128
-BUILT = (3, 5, 7, 8)
+CHUNK = 64
+BUILT = (1, 2, 3, 4, 5, 6, 7, 8)
 
 F32 = jnp.float32
 BF16 = jnp.bfloat16
@@ -68,16 +69,6 @@
     attention_hbm,
     w_value_hbm,
     b_value,
-    w_out_hbm,
-    b_out,
-    gain1,
-    bias1,
-    w_in_hbm,
-    b_in,
-    w_ff_hbm,
-    b_ff,
-    gain2,
-    bias2,
     out,
     gathered,
     values,
@@ -95,9 +86,6 @@
     hot_merged,
     table_merged,
     samp_t,
-    w_out,
-    w_in,
-    w_ff,
     send_sem,
     recv_sem,
     load_sem,
@@ -117,8 +105,8 @@
     has_left, has_right = mine_z > 0, mine_z < line - 1
     cuts = [(begin, min(begin + CHUNK, tokens) - begin) for begin in range(0, tokens, CHUNK)]
 
-    sources = (corners_hbm, bilinear_hbm, attention_hbm, w_value_hbm, w_out_hbm, w_in_hbm, w_ff_hbm)
-    targets = (corners, bilinear, attention, w_value, w_out, w_in, w_ff)
+    sources = (corners_hbm, bilinear_hbm, attention_hbm, w_value_hbm)
+    targets = (corners, bilinear, attention, w_value)
     loads = [
         pltpu.make_async_copy(source, target, load_sem.at[number])
         for number, (source, target) in enumerate(zip(sources, targets))
@@ -203,7 +191,7 @@
                 pl.when(has_right)(right.wait_send)
             across.wait_send()
 
-    for load in loads[:4]:
+    for load in loads:
         load.wait()
     w_value_t[...] = jnp.transpose(w_value[...].astype(F32)).astype(BF16)
     shift_t[...] = jnp.transpose(jnp.broadcast_to(b_value[...], (LANES, model)))
@@ -323,10 +311,21 @@
 
     lax.fori_loop(0, HEADS, blend, 0)
 
-    for load in loads[4:]:
-        load.wait()
-    sampled = jnp.transpose(samp_t[...])[0:tokens, :].astype(BF16)
-    attended = jnp.dot(sampled, w_out[...], preferred_element_type=F32) + b_out[...]
+    out[...] = jnp.transpose(samp_t[...])[0:tokens, :].astype(BF16)
+    finish(me, False, False, own=True)
+    for distance in range(1, line):
+        pl.when(mine_z >= distance)(
+            functools.partial(finish, me - 2 * distance, True, False)
+        )
+        pl.when(mine_z + distance < line)(
+            functools.partial(finish, me + 2 * distance, False, True)
+        )
+
+
+def tail(
+    feat, sampled, w_out, b_out, gain1, bias1, w_in, b_in, w_ff, b_ff, gain2, bias2, out
+):
+    attended = jnp.dot(sampled[...], w_out[...], preferred_element_type=F32) + b_out[...]
     middle = norm(feat[...].astype(F32) + attended, gain1[...], bias1[...]).astype(BF16)
     hidden = jnp.maximum(
         jnp.dot(middle, w_in[...], preferred_element_type=F32) + b_in[...], 0.0
@@ -337,14 +336,6 @@
         + b_ff[...]
     )
     out[...] = norm(result, gain2[...], bias2[...]).astype(BF16)
-    finish(me, False, False, own=True)
-    for distance in range(1, line):
-        pl.when(mine_z >= distance)(
-            functools.partial(finish, me - 2 * distance, True, False)
-        )
-        pl.when(mine_z + distance < line)(
-            functools.partial(finish, me + 2 * distance, False, True)
-        )
 
 
 def body(bands, *args):
@@ -357,11 +348,11 @@
     operands = [
         argument.reshape(1, -1) if argument.ndim == 1 else argument for argument in args
     ]
-    anywhere = {1, 2, 3, 4, 6, 10, 12}
+    anywhere = {1, 2, 3, 4}
     cuts = -(-tokens // CHUNK)
     specs = [
-        pl.BlockSpec(memory_space=pl.ANY if number in anywhere else pltpu.VMEM)
-        for number in range(len(operands))
+        pl.BlockSpec(memory_space=pltpu.HBM if number in anywhere else pltpu.VMEM)
+        for number in range(6)
     ]
     flat_shapes = [
         pltpu.VMEM(
@@ -389,24 +380,37 @@
         pltpu.VMEM((HEADS, 2 * LANES, padded), BF16),
         pltpu.VMEM((HEADS, head_dim, 2 * LANES), BF16),
         pltpu.VMEM((model, padded), F32),
-        pltpu.VMEM(args[6].shape, BF16),
-        pltpu.VMEM(args[10].shape, BF16),
-        pltpu.VMEM(args[12].shape, BF16),
         pltpu.SemaphoreType.DMA((3, bands, cuts)),
         pltpu.SemaphoreType.DMA((bands, cuts)),
         pltpu.SemaphoreType.DMA((len(anywhere),)),
     ] + flat_shapes + table_shapes
-    return pl.pallas_call(
+    held = sum(
+        4 * math.prod(shape.shape) // (2 if shape.dtype == BF16 else 1)
+        for shape in scratch
+        if shape.memory_space == pltpu.VMEM
+    )
+    vmem = pl.BlockSpec(memory_space=pltpu.VMEM)
+    sampled = pl.pallas_call(
         functools.partial(kernel, bands),
         out_shape=jax.ShapeDtypeStruct((tokens, model), BF16),
         in_specs=specs,
-        out_specs=pl.BlockSpec(memory_space=pltpu.VMEM),
+        out_specs=vmem,
         scratch_shapes=scratch,
         compiler_params=pltpu.CompilerParams(
-            collective_id=0, has_side_effects=True, vmem_limit_bytes=60 * 1024 * 1024
+            collective_id=0,
+            has_side_effects=True,
+            vmem_limit_bytes=min(held + 12 * 1024 * 1024, 60 * 1024 * 1024),
         ),
-        name="layer",
-    )(*operands)
+        name="sample",
+    )(*operands[:6])
+    return pl.pallas_call(
+        tail,
+        out_shape=jax.ShapeDtypeStruct((tokens, model), BF16),
+        in_specs=[vmem] * 12,
+        out_specs=vmem,
+        compiler_params=pltpu.CompilerParams(vmem_limit_bytes=24 * 1024 * 1024),
+        name="tail",
+    )(operands[0], sampled, *operands[6:])
 
 
 def solution(mesh):

time: 31.4 us -> 34.8 us (1.11)
  local copies, waits for them, and re-layouts: 1.57 us -> 5.51 us
  Pallas kernels: 29.7 us -> 28.9 us
    unnamed x1 -> x32, local copies, waits for them, and re-layouts: 1.57 us -> 5.51 us
    pallas_call x1, Pallas kernels: 29.7 us -> 27.2 us  [body(): pl.pallas_call(functools.partial(kernel, bands), out_shape=jax.ShapeDtype...]
    pallas_call x0 -> x1, Pallas kernels: none -> 1.71 us  [body(): pl.pallas_call(tail, out_shape=jax.ShapeDtypeStruct((tokens, model), BF16...]
where the time goes in v3:
time: 34.8 us; the launch traced here: 34.5 us
  Pallas kernels  28.9 us (83%)
  local copies, waits for them, and re-layouts  5.51 us (16%)
    pallas_call x1, Pallas kernels, body(): pl.pallas_call(functools.partial(kernel, bands), out_shape=jax.ShapeDtype...  27.2 us
    unnamed x32, local copies, waits for them, and re-layouts  5.51 us
    pallas_call x1, Pallas kernels, body(): pl.pallas_call(tail, out_shape=jax.ShapeDtypeStruct((tokens, model), BF16...  1.71 us

profile of v3, /device:TPU:0, one launch (start us, length us, event | category | flops | bytes accessed | tf_op | source)
XLA Modules:
  0.0 34.5 jit_solution(15478463727455912870)
XLA Ops:
  0.0 0.7 %copy-done.15 = f32[256]{0:T(256)S(1)} copy-done((f32[256]{0:T(256)S(1)}, f32[256]{0:T(256)}, u32[]{:S(2)}) %copy-start.15) | copy-done | bytes 1048
  0.7 1.0 %copy-done.2 = s32[255,512]{1,0:T(8,128)S(1)} copy-done((s32[255,512]{1,0:T(8,128)S(1)}, s32[255,512]{1,0:T(8,128)}, u32[]{:S(2)}) %copy-start.2) | copy-done | bytes 522264
  1.7 1.0 %copy-done.3 = f32[255,512]{1,0:T(8,128)S(1)} copy-done((f32[255,512]{1,0:T(8,128)S(1)}, f32[255,512]{1,0:T(8,128)}, u32[]{:S(2)}) %copy-start.3) | copy-done | bytes 522264
  2.8 0.9 %copy-done.4 = bf16[255,256]{1,0:T(8,128)(2,1)S(1)} copy-done((bf16[255,256]{1,0:T(8,128)(2,1)S(1)}, bf16[255,256]{1,0:T(8,128)(2,1)}, u32[]{:S(2)}) %copy-start.4) | copy-done | bytes 130584
  3.7 0.9 %copy-done.6 = f32[255,128]{1,0:T(8,128)S(1)} copy-done((f32[255,128]{1,0:T(8,128)S(1)}, f32[255,128]{1,0:T(8,128)}, u32[]{:S(2)}) %copy-start.6) | copy-done | bytes 130584
  4.6 0.9 %copy-done.7 = bf16[256,256]{1,0:T(8,128)(2,1)S(1)} copy-done((bf16[256,256]{1,0:T(8,128)(2,1)S(1)}, bf16[256,256]{1,0:T(8,128)(2,1)}, u32[]{:S(2)}) %copy-start.7) | copy-done | bytes 131096
  5.5 0.0 copy-start.9
  5.5 0.0 copy-start.10
  5.5 0.0 copy-start.11
  5.5 0.0 copy-start.12
  5.5 0.0 copy-start.13
  5.5 0.0 copy-start.14
  5.5 27.2 %sample.1.sampled = bf16[255,256]{1,0:T(8,128)(2,1)S(1)} custom-call(bf16[255,256]{1,0:T(8,128)(2,1)S(1)} %copy-done.4, s32[255,512]{1,0:T(8,128)S(1)} %copy-done.2, f32[255,512]{1,0:T(8,128)S(1)} %copy-done.3, f32[255,128]{1,0:T(8,128)S(1)} %copy-done.6, bf16[256,256]{1,0:T(8,128)(2,1)S(1)} %copy-done.7, f32[1,256]{1,0:T(1,128)S(1)} %bitcast.15), custom_call_target="tpu_custom_call" | custom-call | tf_op jit(solution)/shard_map/sample/pallas_call | solution.py:393
  32.7 0.0 copy-done
  32.7 0.0 copy-done.1
  32.7 0.0 copy-done.5
  32.8 0.0 copy-done.8
  32.8 0.0 copy-done.9
  32.8 0.0 copy-done.10
  32.8 0.0 copy-done.11
  32.8 0.0 copy-done.12
  32.8 0.0 copy-done.13
  32.8 0.0 copy-done.14
  32.8 1.7 %tail.1 = bf16[255,256]{1,0:T(8,128)(2,1)} custom-call(bf16[255,256]{1,0:T(8,128)(2,1)S(1)} %copy-done.4, bf16[255,256]{1,0:T(8,128)(2,1)S(1)} %sample.1.sampled, bf16[256,256]{1,0:T(8,128)(2,1)S(1)} %copy-done.5, f32[1,256]{1,0:T(1,128)S(1)} %bitcast.9, f32[1,256]{1,0:T(1,128)S(1)} %bitcast.10, f32[1,256]{1,0:T(1,128)S(1)} %bitcast.11, ...), custom_call_target="tpu_custom_call" | custom-call | tf_op jit(solution)/shard_map/tail/pallas_call | solution.py:406
  (10 shorter events, 0.0 us)
Async XLA Ops:
  0.0 0.7 %copy-start.15 = (f32[256]{0:T(256)S(1)}, f32[256]{0:T(256)}, u32[]{:S(2)}) copy-start(f32[256]{0:T(256)} %param.21) | copy-start | bytes 3076
  0.7 1.0 %copy-start.2 = (s32[255,512]{1,0:T(8,128)S(1)}, s32[255,512]{1,0:T(8,128)}, u32[]{:S(2)}) copy-start(s32[255,512]{1,0:T(8,128)} %corners_hbm.1) | copy-start | bytes 1566724
  1.7 1.0 %copy-start.3 = (f32[255,512]{1,0:T(8,128)S(1)}, f32[255,512]{1,0:T(8,128)}, u32[]{:S(2)}) copy-start(f32[255,512]{1,0:T(8,128)} %bilinear_hbm.1) | copy-start | bytes 1566724
  2.8 0.9 %copy-start.4 = (bf16[255,256]{1,0:T(8,128)(2,1)S(1)}, bf16[255,256]{1,0:T(8,128)(2,1)}, u32[]{:S(2)}) copy-start(bf16[255,256]{1,0:T(8,128)(2,1)} %feat.3) | copy-start | bytes 391684
  3.7 0.9 %copy-start.6 = (f32[255,128]{1,0:T(8,128)S(1)}, f32[255,128]{1,0:T(8,128)}, u32[]{:S(2)}) copy-start(f32[255,128]{1,0:T(8,128)} %attention_hbm.1) | copy-start | bytes 391684
  4.6 0.9 %copy-start.7 = (bf16[256,256]{1,0:T(8,128)(2,1)S(1)}, bf16[256,256]{1,0:T(8,128)(2,1)}, u32[]{:S(2)}) copy-start(bf16[256,256]{1,0:T(8,128)(2,1)} %w_value_hbm.1) | copy-start | bytes 393220
  5.5 27.2 %copy-start = (bf16[256,1024]{1,0:T(8,128)(2,1)S(1)}, bf16[256,1024]{1,0:T(8,128)(2,1)}, u32[]{:S(2)}) copy-start(bf16[256,1024]{1,0:T(8,128)(2,1)} %w_in.1) | copy-start | bytes 1572868
  5.5 27.3 %copy-start.1 = (bf16[1024,256]{1,0:T(8,128)(2,1)S(1)}, bf16[1024,256]{1,0:T(8,128)(2,1)}, u32[]{:S(2)}) copy-start(bf16[1024,256]{1,0:T(8,128)(2,1)} %w_ff.1) | copy-start | bytes 1572868
  5.5 27.3 %copy-start.5 = (bf16[256,256]{1,0:T(8,128)(2,1)S(1)}, bf16[256,256]{1,0:T(8,128)(2,1)}, u32[]{:S(2)}) copy-start(bf16[256,256]{1,0:T(8,128)(2,1)} %w_out.1) | copy-start | bytes 393220
  5.5 27.3 %copy-start.8 = (f32[1024]{0:T(1024)S(1)}, f32[1024]{0:T(1024)}, u32[]{:S(2)}) copy-start(f32[1024]{0:T(1024)} %param.27) | copy-start | bytes 12292
  5.5 27.3 %copy-start.9 = (f32[256]{0:T(256)S(1)}, f32[256]{0:T(256)}, u32[]{:S(2)}) copy-start(f32[256]{0:T(256)} %param.23) | copy-start | bytes 3076
  5.5 27.3 %copy-start.10 = (f32[256]{0:T(256)S(1)}, f32[256]{0:T(256)}, u32[]{:S(2)}) copy-start(f32[256]{0:T(256)} %param.24) | copy-start | bytes 3076
  5.5 27.3 %copy-start.11 = (f32[256]{0:T(256)S(1)}, f32[256]{0:T(256)}, u32[]{:S(2)}) copy-start(f32[256]{0:T(256)} %param.25) | copy-start | bytes 3076
  5.5 27.3 %copy-start.12 = (f32[256]{0:T(256)S(1)}, f32[256]{0:T(256)}, u32[]{:S(2)}) copy-start(f32[256]{0:T(256)} %param.29) | copy-start | bytes 3076
  5.5 27.3 %copy-start.13 = (f32[256]{0:T(256)S(1)}, f32[256]{0:T(256)}, u32[]{:S(2)}) copy-start(f32[256]{0:T(256)} %param.30) | copy-start | bytes 3076
  5.5 27.3 %copy-start.14 = (f32[256]{0:T(256)S(1)}, f32[256]{0:T(256)}, u32[]{:S(2)}) copy-start(f32[256]{0:T(256)} %param.31) | copy-start | bytes 3076

commit v4 on v2

--- a/solution.py
+++ b/solution.py
@@ -14,8 +14,8 @@
 MAP_W = 128
 LANES = 128
 STRIDE = LANES - 1
-CHUNK = 128
-BUILT = (3, 5, 7, 8)
+CHUNK = 64
+BUILT = (1, 2, 3, 4, 5, 6, 7, 8)
 
 F32 = jnp.float32
 BF16 = jnp.bfloat16

time: 31.4 us -> 31.5 us (level)
  no operation moved by 1% of the time
where the time goes in v4:
time: 31.5 us; the launch traced here: 31.4 us
  Pallas kernels  29.8 us (95%)
  local copies, waits for them, and re-layouts  1.57 us (5%)
    pallas_call x1, Pallas kernels, body(): pl.pallas_call(functools.partial(kernel, bands), out_shape=jax.ShapeDtype...  29.8 us
    unnamed x1, local copies, waits for them, and re-layouts  1.57 us

profile of v4, /device:TPU:0, one launch (start us, length us, event | category | flops | bytes accessed | tf_op | source)
XLA Modules:
  0.0 31.4 jit_solution(12008951968247943721)
XLA Ops:
  0.0 29.8 %layer.1 = bf16[255,256]{1,0:T(8,128)(2,1)} custom-call(bf16[255,256]{1,0:T(8,128)(2,1)} %feat.1, s32[255,512]{1,0:T(8,128)} %corners_hbm.1, f32[255,512]{1,0:T(8,128)} %bilinear_hbm.1, f32[255,128]{1,0:T(8,128)} %attention_hbm.1, bf16[256,256]{1,0:T(8,128)(2,1)} %w_value_hbm.1, f32[1,256]{1,0:T(1,128)} %bitcast.9, bf16[256,256]{1,0:T(8,128)(2,1)} %w_out_hbm.1, ...), custom_call_target="tpu_custom_call" | custom-call | tf_op jit(solution)/shard_map/layer/pallas_call | solution.py:399
  29.8 1.6 %copy.18 = bf16[255,256]{1,0:T(8,128)(2,1)} copy(bf16[255,256]{1,0:T(8,128)(2,1)} %layer.1) | data formatting | bytes 261120
